TPU v7x, 16 devices: a whole 2x2x2 slice. The times are simulated.
16 devices in a mesh: ep: 16 (over z, y, x, core).
Axes of the slice: x: 2, y: 2, z: 2, core: 2. Of those that a mesh axis runs over, the one named last changes fastest.
Arguments:
- hidden: bfloat16 [32768, 1024], P('ep')
- grad_out: bfloat16 [32768, 1024], P('ep')
- w_router: bfloat16 [1024, 32], replicated
- b_router: float32 [32], replicated
- expert_ids: int32 [32768, 8], P('ep')
- slot_ids: int32 [32768, 8], P('ep')
- w_gate_up: bfloat16 [32, 1024, 1024], P('ep')
- b_gate_up: float32 [32, 1024], P('ep')
- w_down: bfloat16 [32, 512, 1024], P('ep')
- b_down: float32 [32, 1024], P('ep')
Outputs:
- output 1: bfloat16 [32768, 1024], P('ep')
- output 2: bfloat16 [32768, 1024], P('ep')
- output 3: float32 [1024, 32], replicated
- output 4: float32 [32], replicated
- output 5: float32 [32, 1024, 1024], P('ep')
- output 6: float32 [32, 1024], P('ep')
- output 7: float32 [32, 512, 1024], P('ep')
- output 8: float32 [32, 1024], P('ep')
All inputs are finite; a program needn't handle non-finite values.
Results may differ from a plain program's by a relative error of at most 0.0060219.
Values are sent between devices in bfloat16 or wider.
A program may use at most 1 GiB of HBM per device.

v0:
```python
import jax
import jax.numpy as jnp
from jax import lax
from jax.sharding import PartitionSpec as P

SWIGLU_LIMIT = 7.0
SWIGLU_ALPHA = 1.702


def swiglu(pre_act):
    col_pairs = pre_act.reshape(pre_act.shape[:-1] + (pre_act.shape[-1] // 2, 2))
    gate_in = jnp.minimum(col_pairs[..., 0], SWIGLU_LIMIT)
    up_in = jnp.clip(col_pairs[..., 1], -SWIGLU_LIMIT, SWIGLU_LIMIT)
    return gate_in * jax.nn.sigmoid(SWIGLU_ALPHA * gate_in) * (up_in + 1.0)


def solution(mesh):
    ep_size = mesh.shape['ep']

    def local_block(hidden, grad_out, w_router, b_router, expert_ids, slot_ids, w_gate_up, b_gate_up, w_down, b_down):
        tok_local, d_model = hidden.shape
        top_k = expert_ids.shape[1]
        experts = w_router.shape[1]
        local_experts = w_gate_up.shape[0]
        capacity = (3 * tok_local * top_k + 2 * experts - 1) // (2 * experts)
        buf_rows = experts * capacity
        copy_count = tok_local * top_k
        dest_row = jnp.where(slot_ids >= 0, expert_ids * capacity + slot_ids, buf_rows)
        src_copy = jnp.full((buf_rows + 1,), copy_count, jnp.int32).at[dest_row.reshape(-1)].set(jnp.arange(copy_count, dtype=jnp.int32))[:buf_rows]
        src_tok = src_copy // top_k
        logits = jnp.dot(hidden, w_router, preferred_element_type=jnp.float32) + b_router
        gate_w = jax.nn.softmax(jnp.take_along_axis(logits, expert_ids, axis=1), axis=-1)

        send_x = jnp.take(hidden, src_tok, axis=0, mode='fill', fill_value=0)
        recv_x = lax.all_to_all(send_x, 'ep', 0, 0, tiled=True).reshape(ep_size, local_experts, capacity, d_model)
        pre_act = jnp.einsum('secd,edf->secf', recv_x, w_gate_up, preferred_element_type=jnp.float32) + b_gate_up[None, :, None, :]
        act_val, act_vjp = jax.vjp(swiglu, pre_act)
        act_bf = act_val.astype(jnp.bfloat16)
        y_rows = (jnp.einsum('secf,efd->secd', act_bf, w_down, preferred_element_type=jnp.float32) + b_down[None, :, None, :]).astype(jnp.bfloat16)
        back_y = lax.all_to_all(y_rows.reshape(buf_rows, d_model), 'ep', 0, 0, tiled=True)
        y_copies = jnp.take(back_y, dest_row, axis=0, mode='fill', fill_value=0)
        block_out = jnp.sum(gate_w[:, :, None] * y_copies, axis=1).astype(jnp.bfloat16)

        gate_grad = jnp.einsum('td,tkd->tk', grad_out, y_copies, preferred_element_type=jnp.float32)
        sel_grad = gate_w * (gate_grad - jnp.sum(gate_w * gate_grad, axis=1, keepdims=True))
        expert_range = jnp.arange(experts, dtype=jnp.int32)
        logit_grad = jnp.sum(jnp.where(expert_ids[:, :, None] == expert_range, sel_grad[:, :, None], 0.0), axis=1).astype(jnp.bfloat16)
        row_gate = jnp.take(gate_w.reshape(-1), src_copy, axis=0, mode='fill', fill_value=0)
        row_grad = jnp.take(grad_out, src_tok, axis=0, mode='fill', fill_value=0)
        send_q = (row_gate[:, None] * row_grad).astype(jnp.bfloat16)
        recv_q = lax.all_to_all(send_q, 'ep', 0, 0, tiled=True).reshape(ep_size, local_experts, capacity, d_model)
        grad_b_down = jnp.sum(recv_q, axis=(0, 2), dtype=jnp.float32)
        grad_w_down = jnp.einsum('secf,secd->efd', act_bf, recv_q, preferred_element_type=jnp.float32)
        act_grad = jnp.einsum('secd,efd->secf', recv_q, w_down, preferred_element_type=jnp.float32)
        pre_grad = act_vjp(act_grad)[0].astype(jnp.bfloat16)
        grad_b_gate_up = jnp.sum(pre_grad, axis=(0, 2), dtype=jnp.float32)
        grad_w_gate_up = jnp.einsum('secd,secf->edf', recv_x, pre_grad, preferred_element_type=jnp.float32)
        p_rows = jnp.einsum('secf,edf->secd', pre_grad, w_gate_up, preferred_element_type=jnp.float32).astype(jnp.bfloat16)
        back_p = lax.all_to_all(p_rows.reshape(buf_rows, d_model), 'ep', 0, 0, tiled=True)
        p_copies = jnp.take(back_p, dest_row, axis=0, mode='fill', fill_value=0)
        router_dx = jnp.einsum('te,de->td', logit_grad, w_router, preferred_element_type=jnp.float32)
        grad_hidden = (jnp.sum(p_copies, axis=1, dtype=jnp.float32) + router_dx).astype(jnp.bfloat16)
        grad_w_router = lax.psum(jnp.einsum('td,te->de', hidden, logit_grad, preferred_element_type=jnp.float32), 'ep')
        grad_b_router = lax.psum(jnp.sum(logit_grad, axis=0, dtype=jnp.float32), 'ep')
        return (block_out, grad_hidden, grad_w_router, grad_b_router, grad_w_gate_up, grad_b_gate_up, grad_w_down, grad_b_down)

    tok_spec = P('ep', None)
    in_specs = (tok_spec, tok_spec, P(None, None), P(None), tok_spec, tok_spec, P('ep', None, None), P('ep', None), P('ep', None, None), P('ep', None))
    out_specs = (tok_spec, tok_spec, P(None, None), P(None), P('ep', None, None), P('ep', None), P('ep', None, None), P('ep', None))
    return jax.shard_map(local_block, mesh=mesh, in_specs=in_specs, out_specs=out_specs, check_vma=False)
```

profile of v0, /device:TPU:2, one launch (start us, length us, event | category | flops | bytes accessed | tf_op | source)
XLA Modules:
  0.0 4281.3 jit_solution(17715774583118129459)
XLA Ops:
  7.2 1.7 compare_and_fusion.1
  9.2 0.5 reshape.174
  9.8 60.4 %scatter_custom_fusion = s32[24577]{0:T(1024)S(1)} fusion(s32[16384]{0:T(1024)S(1)} %bitcast.134, s32[16384]{0:T(1024)S(1)} %iota.7, s32[]{:T(128)} %constant.54.clone.1), kind=kCustom, calls=%fused_computation.93 | custom fusion | bytes 98312 | tf_op jit(solution)/shard_map/scatter | solution.py:29
  70.3 0.7 fusion.41
  71.0 122.6 %gather_fusion.2 = bf16[24576,1024]{1,0:T(8,128)(2,1)} fusion(bf16[2048,1024]{1,0:T(8,128)(2,1)} %param.14, s32[24576]{0:T(1024)S(1)} %get-tuple-element.23), kind=kCustom, calls=%fused_computation.clone | custom fusion | bytes 100761600 | tf_op jit(solution)/shard_map/jit(_take)/gather | solution.py:34
  193.6 33.7 broadcast_select_fusion
  227.3 553.2 %all_to_all.42 = bf16[16,1536,1024]{2,1,0:T(8,128)(2,1)} all-to-all(bf16[16,1536,1024]{2,1,0:T(8,128)(2,1)} %bitcast.128), channel_id=1, replica_groups=mesh['ep'=16] {'ep'}, dimensions={0} | all-to-all | bytes 100663296 | tf_op jit(solution)/shard_map/all_to_all | solution.py:35
  780.5 64.7 %add_bitcast_fusion = f32[16,2,768,1024]{3,2,0,1:T(8,128)} fusion(f32[2,1024]{1,0:T(2,128)S(1)} %copy-done.32, bf16[16,2,768,1024]{3,2,1,0:T(8,128)(2,1)} %bitcast.129, bf16[2,1024,1024]{2,1,0:T(8,128)(2,1)} %param.20), kind=kOutput, calls=%fused_computation.12 | convolution fusion | flops 51564773376 | bytes 155197440 | tf_op jit(solution)/shard_map/secd,edf->secf/dot_general | solution.py:36
  845.2 99.9 %copy.107 = f32[16,2,768,1024]{2,0,3,1:T(8,128)} copy(f32[16,2,768,1024]{3,2,0,1:T(8,128)} %add_bitcast_fusion) | data formatting | bytes 201326592 | tf_op jit(solution)/shard_map/add | solution.py:36
  945.1 64.1 %fusion.53 = (f32[16,2,768,512,1]{2,0,4,3,1:T(8,128)}, f32[16,2,768,512,1]{2,0,4,3,1:T(8,128)}) fusion(f32[16,2,768,512,2]{2,0,4,3,1:T(8,128)} %bitcast.7), kind=kLoop, calls=%fused_computation.101 | loop fusion | bytes 201326592 | tf_op jit(solution)/shard_map/jvp()/slice | solution.py:12
  1009.2 65.0 %fusion.7 = bf16[16,2,768,512]{2,3,0,1:T(8,128)(2,1)} fusion(f32[16,2,768,512,1]{2,0,4,3,1:T(8,128)} %get-tuple-element.21, f32[16,2,768,512,1]{2,0,4,3,1:T(8,128)} %get-tuple-element.20), kind=kLoop, calls=%fused_computation.28 | loop fusion | flops 125829120 | bytes 125829120 | tf_op jit(solution)/shard_map/convert_element_type | solution.py:38
  1074.2 34.6 fusion.5
  1108.8 33.2 copy.111
  1142.1 5.7 all-to-all-start.1
  1147.8 1.1 copy.104
  1148.8 0.3 copy.112
  1149.2 1.1 reshape.246
  1150.6 0.5 reshape.218
  1151.1 3.5 convolution_add_fusion
  1154.7 130.6 %gather_fusion.1 = f32[16384]{0:T(1024)S(1)} fusion(f32[2048,32]{0,1:T(8,128)S(1)} %convolution_add_fusion, s32[16384]{0:T(1024)S(1)} %reshape.218), kind=kCustom, calls=%fused_computation.5 | custom fusion | bytes 262144 | tf_op jit(solution)/shard_map/jit(take_along_axis)/gather | solution.py:32
  1285.2 0.6 reshape.221
  1286.1 125.0 %gather_fusion.4 = bf16[24576,1024]{1,0:T(8,128)(2,1)} fusion(bf16[2048,1024]{1,0:T(8,128)(2,1)} %param.15, s32[24576]{0:T(1024)} %copy-done.16), kind=kCustom, calls=%fused_computation.2.clone | custom fusion | bytes 100761600 | tf_op jit(solution)/shard_map/jit(_take)/gather | solution.py:49
  1411.2 336.8 %all-to-all-done.1 = bf16[16,1536,1024]{2,1,0:T(8,128)(2,1)} async-done(((bf16[16,1536,1024]{2,1,0:T(8,128)(2,1)}), bf16[16,1536,1024]{2,1,0:T(8,128)(2,1)}, u32[]{:S(2)}, u32[]{:S(2)}) %all-to-all-start.1) | async-done | bytes 50331680 | tf_op jit(solution)/shard_map/all_to_all | solution.py:40
  1748.0 319.0 %gather_fusion.3 = bf16[16384,1024]{1,0:T(8,128)(2,1)} fusion(bf16[24576,1024]{1,0:T(8,128)(2,1)} %bitcast.14, s32[16384]{0:T(1024)S(1)} %broadcast_clamp_fusion.1), kind=kCustom, calls=%fused_computation.1.clone | custom fusion | bytes 67174400 | tf_op jit(solution)/shard_map/jit(_take)/gather | solution.py:41
  2067.1 25.7 fusion.24
  2092.8 0.5 copy.128
  2093.3 0.6 fusion.42
  2094.3 0.5 div.36
  2094.8 135.8 %gather_fusion = f32[24576]{0:T(1024)S(1)} fusion(f32[16384]{0:T(1024)S(1)} %div.36, s32[24576]{0:T(1024)} %get-tuple-element.22), kind=kCustom, calls=%fused_computation.4 | custom fusion | bytes 294912 | tf_op jit(solution)/shard_map/jit(_take)/gather | solution.py:48
  2230.7 33.6 multiply_convert_fusion
  2264.3 569.7 %all_to_all.43 = bf16[16,1536,1024]{2,1,0:T(8,128)(2,1)} all-to-all(bf16[16,1536,1024]{2,1,0:T(8,128)(2,1)} %bitcast.127), channel_id=1, replica_groups=mesh['ep'=16] {'ep'}, dimensions={0} | all-to-all | bytes 100663296 | tf_op jit(solution)/shard_map/all_to_all | solution.py:51
  2834.0 96.9 %fusion.6 = (f32[16,2,768,512,1]{2,3,0,1,4:T(8,128)}, f32[16,2,768,512,1]{2,3,0,1,4:T(8,128)}) fusion(f32[16,2,768,512,1]{2,0,4,3,1:T(8,128)} %get-tuple-element.21, f32[16,2,768,512,1]{2,0,4,3,1:T(8,128)} %get-tuple-element.20, bf16[2,512,1024]{2,1,0:T(8,128)(2,1)S(1)} %copy-done, bf16[16,2,768,1024]{3,2,1,0:T(8,128)(2,1)} %bitcast.123), kind=kOutput, calls=%fused_computation.23 | convolution fusion | flops 26185039872 | bytes 253755392 | tf_op jit(solution)/shard_map/secd,efd->secf/dot_general | solution.py:54
  2930.9 49.8 %convert_reduce_fusion.1 = (f32[2,512,2]{1,0,2:T(2,128)}, bf16[16,2,768,512,2]{2,3,0,1,4:T(8,128)(2,1)}) fusion(f32[16,2,768,512,1]{2,3,0,1,4:T(8,128)} %get-tuple-element.19, f32[16,2,768,512,1]{2,3,0,1,4:T(8,128)} %get-tuple-element.18), kind=kLoop, calls=%fused_computation.8 | loop fusion | flops 100661248 | bytes 151003136 | tf_op jit(solution)/shard_map/reduce_sum | solution.py:56
  2980.7 45.8 %copy.116 = bf16[16,2,768,512,2]{2,0,4,3,1:T(8,128)(2,1)} copy(bf16[16,2,768,512,2]{2,3,0,1,4:T(8,128)(2,1)} %get-tuple-element.13) | data formatting | bytes 100663296 | tf_op jit(solution)/shard_map/convert_element_type | solution.py:55
  3026.5 78.3 %convert_bitcast_fusion = bf16[16,2,768,1024]{3,2,0,1:T(8,128)(2,1)} fusion(bf16[16,2,768,1024]{2,0,3,1:T(8,128)(2,1)} %bitcast.131, bf16[2,1024,1024]{2,1,0:T(8,128)(2,1)} %param.20), kind=kOutput, calls=%fused_computation.42 | convolution fusion | flops 51564773376 | bytes 104857600 | tf_op jit(solution)/shard_map/secf,edf->secd/dot_general | solution.py:58
  3104.8 33.5 copy.118
  3138.3 5.4 all-to-all-start.3
  3144.1 623.2 %psum.15 = f32[32]{0:T(128)} all-reduce(f32[32]{0:T(128)S(1)} %convert_reduce_fusion.3), channel_id=1, replica_groups=mesh['ep'=16] {'ep'}, use_global_device_ids=true, to_apply=%region_9.12 | all-reduce | flops 32 | bytes 256 | tf_op jit(solution)/shard_map/psum | solution.py:64
  3767.3 3.7 convolution_bitcast_fusion
  3771.3 0.9 reduce_sum.88
  3772.2 19.2 convert_reduce_fusion
  3791.4 3.7 reduce_sum.91
  3795.1 35.2 fusion.34
  3830.3 69.7 %fusion.31 = f32[2,1024,1024]{2,1,0:T(8,128)} fusion(bf16[16,2,768,1024]{3,2,1,0:T(8,128)(2,1)} %bitcast.130, bf16[16,2,768,1024]{2,0,3,1:T(8,128)(2,1)} %bitcast.132), kind=kOutput, calls=%fused_computation.58 | convolution fusion | flops 51539607552 | bytes 109051904 | tf_op jit(solution)/shard_map/secd,secf->edf/dot_general | solution.py:57
  3900.0 319.7 %gather_fusion.5 = bf16[16384,1024]{1,0:T(8,128)(2,1)} fusion(bf16[24576,1024]{1,0:T(8,128)(2,1)} %bitcast.29, s32[16384]{0:T(1024)S(1)} %copy-done.2), kind=kCustom, calls=%fused_computation.3.clone | custom fusion | bytes 67174400 | tf_op jit(solution)/shard_map/jit(_take)/gather | solution.py:60
  4219.7 49.6 %convert_reduce_fusion.2 = (f32[2048,1024]{1,0:T(8,128)S(1)}, bf16[2048,1024]{1,0:T(8,128)(2,1)}) fusion(bf16[16384,1024]{1,0:T(8,128)(2,1)} %gather_fusion.5, pred[2048,8]{1,0:T(8,128)(4,1)S(1)} %copy-done.13, bf16[16384,1024]{1,0:T(8,128)(2,1)} %gather_fusion.3, f32[2048,8]{1,0:T(8,128)S(1)} %copy-done.4), kind=kLoop, calls=%fused_computation.14 | loop fusion | flops 113246208 | bytes 79773696 | tf_op jit(solution)/shard_map/reduce_sum | solution.py:62
  4269.3 3.3 add_convert_fusion.2
  4272.6 1.6 copy.172
  (89 shorter events, 2.4 us)
Async XLA Ops:
  7.2 1067.0 %copy-start = (bf16[2,512,1024]{2,1,0:T(8,128)(2,1)S(1)}, bf16[2,512,1024]{2,1,0:T(8,128)(2,1)}, u32[]{:S(2)}) copy-start(bf16[2,512,1024]{2,1,0:T(8,128)(2,1)} %param.22) | copy-start | bytes 6291460
  8.8 184.7 %copy-start.21 = (s32[2048,8]{0,1:T(8,128)}, s32[2048,8]{0,1:T(8,128)S(1)}, u32[]{:S(2)}) copy-start(s32[2048,8]{0,1:T(8,128)S(1)} %get-tuple-element.17) | copy-start | bytes 196612
  70.2 123.4 %copy-start.10 = (s32[24577]{0:T(1024)}, s32[24577]{0:T(1024)S(1)}, u32[]{:S(2)}) copy-start(s32[24577]{0:T(1024)S(1)} %scatter_custom_fusion) | copy-start | bytes 294928
  70.3 123.3 %copy-start.26 = (pred[24576]{0:T(1024)(128)(4,1)}, pred[24576]{0:T(1024)(128)(4,1)S(1)}, u32[]{:S(2)}) copy-start(pred[24576]{0:T(1024)(128)(4,1)S(1)} %compare_and_fusion) | copy-start | bytes 73732
  71.0 122.6 %copy-start.16 = (s32[24576]{0:T(1024)}, s32[24576]{0:T(1024)S(1)}, u32[]{:S(2)}) copy-start(s32[24576]{0:T(1024)S(1)} %get-tuple-element.23) | copy-start | bytes 294916
  227.3 553.2 %copy-start.32 = (f32[2,1024]{1,0:T(2,128)S(1)}, f32[2,1024]{1,0:T(2,128)}, u32[]{:S(2)}) copy-start(f32[2,1024]{1,0:T(2,128)} %param.21) | copy-start | bytes 24580
  1009.2 65.0 %copy-start.33 = (f32[2,1024]{1,0:T(2,128)S(1)}, f32[2,1024]{1,0:T(2,128)}, u32[]{:S(2)}) copy-start(f32[2,1024]{1,0:T(2,128)} %param.23) | copy-start | bytes 24580
  1142.0 5.7 copy-start.28
  1142.0 6.8 copy-start.22
  1142.1 8.2 copy-start.5
  1142.1 9.1 copy-start.23
  1142.1 9.0 copy-start.31
  1142.1 605.9 %all-to-all-start.1 = ((bf16[16,1536,1024]{2,1,0:T(8,128)(2,1)}), bf16[16,1536,1024]{2,1,0:T(8,128)(2,1)}, u32[]{:S(2)}, u32[]{:S(2)}) async-start(bf16[16,1536,1024]{2,1,0:T(8,128)(2,1)} %bitcast.126), calls=%async_computation.1 | async-start | bytes 100663296 | tf_op jit(solution)/shard_map/all_to_all | solution.py:40
  1286.1 125.0 %copy-start.14 = (f32[2048,8]{0,1:T(8,128)}, f32[2048,8]{0,1:T(8,128)S(1)}, u32[]{:S(2)}) copy-start(f32[2048,8]{0,1:T(8,128)S(1)} %copy.102) | copy-start | bytes 196612
  1286.1 125.0 %copy-start.6 = (s32[2048,8]{0,1:T(8,128)S(1)}, s32[2048,8]{0,1:T(8,128)}, u32[]{:S(2)}) copy-start(s32[2048,8]{0,1:T(8,128)} %param.18) | copy-start | bytes 196612
  1286.1 125.1 %copy-start.25 = (s32[16384]{0:T(1024)S(1)}, s32[16384]{0:T(1024)}, u32[]{:S(2)}) copy-start(s32[16384]{0:T(1024)} %reshape.246) | copy-start | bytes 196612
  1411.2 655.8 %copy-start.1 = (s32[16384]{0:T(1024)}, s32[16384]{0:T(1024)S(1)}, u32[]{:S(2)}) copy-start(s32[16384]{0:T(1024)S(1)} %broadcast_clamp_fusion.1) | copy-start | bytes 196612
  1748.0 319.0 %copy-start.12 = (pred[2048,8]{1,0:T(8,128)(4,1)S(1)}, pred[2048,8]{1,0:T(8,128)(4,1)}, u32[]{:S(2)}) copy-start(pred[2048,8]{1,0:T(8,128)(4,1)} %copy.104) | copy-start | bytes 49156
  2067.1 26.2 copy-start.15
  2093.3 0.7 copy-start.17
  2093.9 0.9 copy-start.19
  2094.3 136.4 %copy-start.3 = (f32[2048,8]{1,0:T(8,128)}, f32[2048,8]{1,0:T(8,128)S(1)}, u32[]{:S(2)}) copy-start(f32[2048,8]{1,0:T(8,128)S(1)} %copy.103) | copy-start | bytes 196612
  2094.8 135.8 %copy-start.11 = (s32[24577]{0:T(1024)S(1)}, s32[24577]{0:T(1024)}, u32[]{:S(2)}) copy-start(s32[24577]{0:T(1024)} %copy-done.10) | copy-start | bytes 294928
  2094.8 135.9 %copy-start.27 = (pred[24576]{0:T(1024)(128)(4,1)S(1)}, pred[24576]{0:T(1024)(128)(4,1)}, u32[]{:S(2)}) copy-start(pred[24576]{0:T(1024)(128)(4,1)} %copy-done.26) | copy-start | bytes 73732
  3138.2 5.5 copy-start.18
  3138.2 5.5 copy-start.20
  3138.3 5.5 copy-start.30
  3138.3 5.5 copy-start.7
  3138.3 632.8 %copy-start.29 = (f32[2,512,2]{1,0,2:T(2,128)S(1)}, f32[2,512,2]{1,0,2:T(2,128)}, u32[]{:S(2)}) copy-start(f32[2,512,2]{1,0,2:T(2,128)} %get-tuple-element.12) | copy-start | bytes 24580
  3138.3 761.7 %all-to-all-start.3 = ((bf16[16,1536,1024]{2,1,0:T(8,128)(2,1)}), bf16[16,1536,1024]{2,1,0:T(8,128)(2,1)}, u32[]{:S(2)}, u32[]{:S(2)}) async-start(bf16[16,1536,1024]{2,1,0:T(8,128)(2,1)} %bitcast.125), calls=%async_computation.3 | async-start | bytes 100663296 | tf_op jit(solution)/shard_map/all_to_all | solution.py:59
  3143.7 1128.9 %all-reduce.4.cloned.1.call-start = ((), (), s32[]{:S(2)}) async-start(), calls=%async_computation.4 | async-start | bytes 262144 | tf_op jit(solution)/shard_map/psum | solution.py:63
  3144.0 686.3 %copy-start.8 = (bf16[2048,32]{0,1:T(8,128)(2,1)}, bf16[2048,32]{0,1:T(8,128)(2,1)S(1)}, u32[]{:S(2)}) copy-start(bf16[2048,32]{0,1:T(8,128)(2,1)S(1)} %select_reduce_fusion) | copy-start | bytes 393220
  3830.3 69.7 %copy-start.2 = (s32[16384]{0:T(1024)S(1)}, s32[16384]{0:T(1024)}, u32[]{:S(2)}) copy-start(s32[16384]{0:T(1024)} %copy-done.1) | copy-start | bytes 196612
  3900.0 319.7 %copy-start.4 = (f32[2048,8]{1,0:T(8,128)S(1)}, f32[2048,8]{1,0:T(8,128)}, u32[]{:S(2)}) copy-start(f32[2048,8]{1,0:T(8,128)} %copy-done.3) | copy-start | bytes 196612
  3900.0 319.7 %copy-start.13 = (pred[2048,8]{1,0:T(8,128)(4,1)S(1)}, pred[2048,8]{1,0:T(8,128)(4,1)}, u32[]{:S(2)}) copy-start(pred[2048,8]{1,0:T(8,128)(4,1)} %copy.104) | copy-start | bytes 49156
  4219.7 49.6 %copy-start.9 = (bf16[2048,32]{0,1:T(8,128)(2,1)S(1)}, bf16[2048,32]{0,1:T(8,128)(2,1)}, u32[]{:S(2)}) copy-start(bf16[2048,32]{0,1:T(8,128)(2,1)} %copy-done.8) | copy-start | bytes 393220
  4219.7 49.6 %copy-start.24 = (bf16[1024,32]{0,1:T(8,128)(2,1)S(1)}, bf16[1024,32]{0,1:T(8,128)(2,1)}, u32[]{:S(2)}) copy-start(bf16[1024,32]{0,1:T(8,128)(2,1)} %param.16) | copy-start | bytes 196612
Sparse Core Ops, SparseCore 0:
  3771.2 64.5 all-reduce.3
where the time goes:
time: 4300 us; the launch traced here: 4280 us
  blocking collectives  1750 us (41%)
  local copies, waits for them, and re-layouts  1500 us (35%)
  matrix products  416 us (10%)
  waiting for transfers between devices  337 us (8%)
  other arithmetic  258 us (6%)
    psum x1, blocking collectives, local_block(): lax.psum(jnp.sum(logit_grad, axis=0, dtype=jnp.float32), 'ep')  623 us
    all_to_all x1, blocking collectives, local_block(): lax.all_to_all(send_q, 'ep', 0, 0, tiled=True)  570 us
    all_to_all x1, blocking collectives, local_block(): lax.all_to_all(send_x, 'ep', 0, 0, tiled=True)  553 us
    all_to_all x1, waiting for transfers between devices, local_block(): lax.all_to_all(y_rows.reshape(buf_rows, d_model), 'ep', 0, 0, tiled=True)  337 us
    gather x1, local copies, waits for them, and re-layouts, local_block(): p_copies = jnp.take(back_p, dest_row, axis=0, mode='fill', fill_value=0)  320 us
    gather x1, local copies, waits for them, and re-layouts, local_block(): y_copies = jnp.take(back_y, dest_row, axis=0, mode='fill', fill_value=0)  319 us
    gather x1, local copies, waits for them, and re-layouts, local_block(): jnp.take(gate_w.reshape(-1), src_copy, axis=0, mode='fill', fill_value=0)  136 us
    gather x5, local copies, waits for them, and re-layouts, local_block(): jnp.take_along_axis(logits, expert_ids, axis=1)  132 us
  transfers between devices with their start and end apart: 3, of which 1 were waited for; matrix products, arithmetic and copies ran while one was open for 18% of the time, Pallas kernels for 0%

commit v1 on v0

v1 whole, which is shorter than its diff:
```python
import functools
import jax
import jax.numpy as jnp
from jax import lax
from jax.experimental import pallas as pl
from jax.experimental.pallas import tpu as pltpu
from jax.sharding import PartitionSpec as P

SWIGLU_LIMIT = 7.0
SWIGLU_ALPHA = 1.702
TILE = 512
F32 = jnp.float32
BF16 = jnp.bfloat16


def dot(a, b, ca, cb):
    return lax.dot_general(a, b, (((ca,), (cb,)), ((), ())), preferred_element_type=F32)


def expert_kernel(tile, lane0, has_acc, has_grad, *refs):
    it = iter(refs)
    x_ref, dy_ref, gate_ref, w_ref, b_ref = (next(it) for _ in range(5))
    acc_refs = [next(it) for _ in range(2)] if has_acc else []
    gin_ref = next(it) if has_grad else None
    out_ref, dx_ref, r_ref, grad_ref = (next(it) for _ in range(4))
    acc_sem = next(it) if has_acc else None
    gbuf_ref, grad_sem = (next(it), next(it)) if has_grad else (None, None)
    expert = pl.program_id(0)
    tokens, d_model = x_ref.shape
    ff = d_model // 2

    @pl.when(expert == 0)
    def _():
        if has_acc:
            loads = [pltpu.make_async_copy(src, dst, acc_sem.at[n]) for n, (src, dst) in enumerate(zip(acc_refs, (out_ref, dx_ref)))]
            for load in loads:
                load.start()
        r_ref[...] = jnp.zeros_like(r_ref)
        if has_grad:
            pltpu.make_async_copy(gin_ref.at[0], gbuf_ref, grad_sem).start()
        if has_acc:
            for load in loads:
                load.wait()
        else:
            out_ref[...] = jnp.zeros_like(out_ref)
            dx_ref[...] = jnp.zeros_like(dx_ref)

    if has_grad:
        pltpu.make_async_copy(gin_ref.at[expert], gbuf_ref, grad_sem).wait()
        grad_ref[0] = gbuf_ref[...]

        @pl.when(expert + 1 < pl.num_programs(0))
        def _():
            pltpu.make_async_copy(gin_ref.at[expert + 1], gbuf_ref, grad_sem).start()
    else:
        grad_ref[...] = jnp.zeros_like(grad_ref)

    def body(i, carry):
        rows = pl.ds(pl.multiple_of(i * tile, tile), tile)
        x = x_ref[rows, :]
        dy = dy_ref[rows, :]
        gates = gate_ref[rows, :]
        lane = lax.broadcasted_iota(jnp.int32, gates.shape, 1)
        here = lane == expert + lane0
        w = jnp.sum(jnp.where(here, gates, 0.0), axis=1, keepdims=True)
        dyf = dy.astype(F32)
        q = (w * dyf).astype(BF16)
        hg = dot(x, w_ref[0, :d_model, :ff], 1, 0) + b_ref[0, 0:1, :ff]
        hu = dot(x, w_ref[0, :d_model, ff:], 1, 0) + b_ref[0, 0:1, ff:]
        g = jnp.minimum(hg, SWIGLU_LIMIT)
        u = jnp.clip(hu, -SWIGLU_LIMIT, SWIGLU_LIMIT)
        u1 = u + 1.0
        s = 1.0 / (1.0 + jnp.exp(-SWIGLU_ALPHA * g))
        gs = g * s
        act = (gs * u1).astype(BF16)
        da = dot(q, w_ref[0, d_model:, :], 1, 1)
        y = (dot(act, w_ref[0, d_model:, :], 1, 0) + b_ref[0, 1:2, :]).astype(BF16).astype(F32)
        r = jnp.sum(y * dyf, axis=1, keepdims=True)
        r_ref[rows, :] = jnp.where(here, r, r_ref[rows, :])
        out_ref[rows, :] += w * y
        g_pass = jnp.where(hg < SWIGLU_LIMIT, 1.0, jnp.where(hg == SWIGLU_LIMIT, 0.5, 0.0))
        mag = jnp.abs(hu)
        u_pass = jnp.where(mag < SWIGLU_LIMIT, 1.0, jnp.where(mag == SWIGLU_LIMIT, 0.5, 0.0))
        dg = (da * u1 * (s + SWIGLU_ALPHA * gs * (1.0 - s)) * g_pass).astype(BF16)
        du = (da * gs * u_pass).astype(BF16)
        p = dot(dg, w_ref[0, :d_model, :ff], 1, 1) + dot(du, w_ref[0, :d_model, ff:], 1, 1)
        dx_ref[rows, :] += p.astype(BF16).astype(F32)
        grad_ref[0, :d_model, :ff] += dot(x, dg, 0, 0)
        grad_ref[0, :d_model, ff:] += dot(x, du, 0, 0)
        grad_ref[0, d_model:d_model + ff, :] += dot(act, q, 0, 0)
        row = d_model + ff
        grad_ref[0, row:row + 1, :ff] += jnp.sum(dg.astype(F32), axis=0, keepdims=True)
        grad_ref[0, row:row + 1, ff:] += jnp.sum(du.astype(F32), axis=0, keepdims=True)
        grad_ref[0, row + 1:row + 2, :] += jnp.sum(q.astype(F32), axis=0, keepdims=True)
        return carry

    lax.fori_loop(0, tokens // tile, body, 0)


def run_experts(lane0, x, dy, gates, weights, bias, acc=None, grad_in=None):
    tokens, d_model = x.shape
    experts, w_rows, _ = weights.shape
    g_rows = w_rows + 8
    once = lambda e: (0, 0)
    per = lambda e: (e, 0, 0)
    keep = pl.Buffered(1)
    full = lambda a: pl.BlockSpec(a.shape, once, pipeline_mode=keep)
    args = [x, dy, gates, weights, bias]
    specs = [full(x), full(dy), full(gates), pl.BlockSpec((1, w_rows, d_model), per), pl.BlockSpec((1, 2, d_model), per)]
    scratch = []
    if acc is not None:
        args += list(acc)
        specs += [pl.BlockSpec(memory_space=pl.ANY)] * 2
        scratch.append(pltpu.SemaphoreType.DMA((2,)))
    if grad_in is not None:
        args.append(grad_in)
        specs.append(pl.BlockSpec(memory_space=pl.ANY))
        scratch += [pltpu.VMEM((g_rows, d_model), F32), pltpu.SemaphoreType.DMA]
    tok_f32 = jax.ShapeDtypeStruct((tokens, d_model), F32)
    out_shape = [tok_f32, tok_f32, jax.ShapeDtypeStruct(gates.shape, F32), jax.ShapeDtypeStruct((experts, g_rows, d_model), F32)]
    out_specs = [pl.BlockSpec((tokens, d_model), once, pipeline_mode=keep)] * 2 + [pl.BlockSpec(gates.shape, once, pipeline_mode=keep), pl.BlockSpec((1, g_rows, d_model), per)]
    flops = 2 * experts * tokens * d_model * d_model * 9 // 2
    return pl.pallas_call(
        functools.partial(expert_kernel, min(TILE, tokens), lane0, acc is not None, grad_in is not None),
        grid=(experts,), in_specs=specs, out_specs=out_specs, out_shape=out_shape, scratch_shapes=scratch,
        compiler_params=pltpu.CompilerParams(dimension_semantics=("arbitrary",), vmem_limit_bytes=67043328),
        cost_estimate=pl.CostEstimate(flops=flops, bytes_accessed=experts * (w_rows * 2 + g_rows * 4) * d_model + tokens * d_model * 20, transcendentals=0),
        name="experts",
    )(*args)


def solution(mesh):
    ep_size = mesh.shape['ep']
    group = ep_size // 2
    groups = [list(range(group)), list(range(group, ep_size))]
    swap = [(i, (i + group) % ep_size) for i in range(ep_size)]

    def gather(a):
        return lax.all_gather(a, 'ep', axis=0, tiled=True, axis_index_groups=groups)

    def scatter(a):
        return lax.psum_scatter(a, 'ep', scatter_dimension=0, tiled=True, axis_index_groups=groups)

    def exchange(a):
        return lax.ppermute(a, 'ep', swap)

    def local_block(hidden, grad_out, w_router, b_router, expert_ids, slot_ids, w_gate_up, b_gate_up, w_down, b_down):
        tok, d_model = hidden.shape
        top_k = expert_ids.shape[1]
        experts = w_router.shape[1]
        local = w_gate_up.shape[0]
        ff = w_down.shape[1]
        half = experts // 2
        upper = lax.axis_index('ep') >= group

        src = lax.broadcasted_iota(jnp.int32, (2 * ff, 2 * ff), 0)
        dst = lax.broadcasted_iota(jnp.int32, (2 * ff, 2 * ff), 1)
        apart = (src == 2 * (dst % ff) + dst // ff)
        w_cat = [jnp.concatenate([jnp.dot(w_gate_up[c], apart.astype(BF16), preferred_element_type=F32).astype(BF16), w_down[c]], axis=0)[None] for c in range(local)]
        bias = jnp.stack([b_gate_up.reshape(local, ff, 2).transpose(0, 2, 1).reshape(local, 2 * ff), b_down], axis=1)
        w_all = [gather(w) for w in w_cat]
        b_all = gather(bias).reshape(group, local, 2, d_model)

        def order(a):
            return a.reshape(a.shape[:-1] + (2, group, local)).swapaxes(-1, -2).reshape(a.shape)

        def unorder(a):
            return a.reshape(a.shape[:-1] + (2, local, group)).swapaxes(-1, -2).reshape(a.shape)

        w_rt = order(w_router)
        ids = order(jnp.arange(experts, dtype=jnp.int32))
        logits = jnp.dot(hidden, w_rt, preferred_element_type=F32) + order(b_router)
        chosen = jnp.zeros((tok, experts), bool)
        kept = jnp.zeros((tok, experts), bool)
        for k in range(top_k):
            hit = expert_ids[:, k:k + 1] == ids[None, :]
            chosen = chosen | hit
            kept = kept | (hit & (slot_ids[:, k:k + 1] >= 0))
        top = jnp.max(jnp.where(chosen, logits, -jnp.inf), axis=1, keepdims=True)
        expo = jnp.where(chosen, jnp.exp(jnp.where(chosen, logits - top, 0.0)), 0.0)
        gate = expo / jnp.sum(expo, axis=1, keepdims=True)
        gate_kept = jnp.where(kept, gate, 0.0)
        lower_cols, upper_cols = gate_kept[:, :half], gate_kept[:, half:]
        pad = lambda a: jnp.pad(a, ((0, 0), (0, 128 - half)))
        g_own = pad(jnp.where(upper, upper_cols, lower_cols))
        x_far = exchange(hidden)
        dy_far = exchange(grad_out)
        g_far = exchange(pad(jnp.where(upper, lower_cols, upper_cols)))

        out_1, dx_1, r_1, gr_1 = run_experts(0, hidden, grad_out, g_own, w_all[0], b_all[:, 0])
        out_2, dx_2, r_2, gr_a = run_experts(0, x_far, dy_far, g_far, w_all[0], b_all[:, 0], grad_in=gr_1)
        part_a = scatter(gr_a)
        out_3, dx_3, r_3, gr_3 = run_experts(group, x_far, dy_far, g_far, w_all[1], b_all[:, 1], acc=(out_2, dx_2))
        r_far = exchange(r_2 + r_3)
        dx_far = exchange(dx_3)
        out_far = exchange(out_3)
        out_4, dx_4, r_4, gr_b = run_experts(group, hidden, grad_out, g_own, w_all[1], b_all[:, 1], acc=(out_1, dx_1), grad_in=gr_3)
        part_b = scatter(gr_b)

        block_out = (out_4 + out_far).astype(BF16)
        r_own = (r_1 + r_4)[:, :half]
        r_oth = r_far[:, :half]
        gate_grad = jnp.where(kept, jnp.concatenate([jnp.where(upper, r_oth, r_own), jnp.where(upper, r_own, r_oth)], axis=1), 0.0)
        sel_grad = gate * (gate_grad - jnp.sum(gate * gate_grad, axis=1, keepdims=True))
        logit_grad = sel_grad.astype(BF16)
        router_dx = jnp.einsum('te,de->td', logit_grad, w_rt, preferred_element_type=F32)
        grad_hidden = (dx_4 + dx_far + router_dx).astype(BF16)
        grad_rt = jnp.concatenate([jnp.einsum('te,td->ed', logit_grad, hidden, preferred_element_type=F32), jnp.pad(jnp.sum(logit_grad, axis=0, dtype=F32)[None], ((0, 7), (0, d_model - experts)))], axis=0)
        step = 1
        while step < ep_size:
            grad_rt = grad_rt + lax.ppermute(grad_rt, 'ep', [(i, i ^ step) for i in range(ep_size)])
            step *= 2
        grad_w_router = unorder(lax.optimization_barrier(grad_rt[:experts].T))
        grad_b_router = unorder(grad_rt[experts, :experts])

        def together(part):
            return lax.dot_general(part[0, :d_model], apart.astype(F32), (((1,), (1,)), ((), ())), precision=lax.Precision.HIGHEST, preferred_element_type=F32)

        parts = (part_a, part_b)
        row = d_model + ff
        grad_w_gate_up = jnp.stack([together(p) for p in parts])
        grad_w_down = jnp.stack([p[0, d_model:row] for p in parts])
        grad_b_gate_up = jnp.stack([p[0, row].reshape(2, ff).T.reshape(2 * ff) for p in parts])
        grad_b_down = jnp.stack([p[0, row + 1] for p in parts])
        return (block_out, grad_hidden, grad_w_router, grad_b_router, grad_w_gate_up, grad_b_gate_up, grad_w_down, grad_b_down)

    tok_spec = P('ep', None)
    in_specs = (tok_spec, tok_spec, P(None, None), P(None), tok_spec, tok_spec, P('ep', None, None), P('ep', None), P('ep', None, None), P('ep', None))
    out_specs = (tok_spec, tok_spec, P(None, None), P(None), P('ep', None, None), P('ep', None), P('ep', None, None), P('ep', None))
    return jax.shard_map(local_block, mesh=mesh, in_specs=in_specs, out_specs=out_specs, check_vma=False)
```

time: 4300 us -> 1500 us (0.35)
  blocking collectives: 1750 us -> 10.1 us
  local copies, waits for them, and re-layouts: 1500 us -> 13.6 us
  Pallas kernels: 0 us -> 873 us
  matrix products: 416 us -> 39.9 us
  other arithmetic: 258 us -> 44.6 us
  waiting for transfers between devices: 337 us -> 479 us
    gather x10 -> x0, local copies, waits for them, and re-layouts: 1150 us -> none  [the longest x1 320 us: local_block(): p_copies = jnp.take(back_p, dest_row, axis=0, mode='fill', fill_value=0)]
    all_to_all x2 -> x0, blocking collectives: 1120 us -> none  [the longest x1 570 us: local_block(): lax.all_to_all(send_q, 'ep', 0, 0, tiled=True)]
    pallas_call x0 -> x4, Pallas kernels: none -> 873 us  [run_experts(): pl.pallas_call(functools.partial(expert_kernel, min(TILE, tokens), lane0,...]
    psum x1 -> x0, blocking collectives: 623 us -> none  [local_block(): lax.psum(jnp.sum(logit_grad, axis=0, dtype=jnp.float32), 'ep')]
    ppermute x0 -> x10, waiting for transfers between devices: none -> 397 us  [the longest x6 381 us: exchange(): return lax.ppermute(a, 'ep', swap)]
    dot_general x10 -> x7, matrix products: 416 us -> 39.9 us  [the longest x2 16.4 us: together(): lax.dot_general(part[0, :d_model], apart.astype(F32), (((1,), (1,)), ((),...]
    all_to_all x2 -> x0, waiting for transfers between devices: 337 us -> none  [the longest x1 337 us: local_block(): lax.all_to_all(y_rows.reshape(buf_rows, d_model), 'ep', 0, 0, tiled=True)]
    convert_element_type x3 -> x0, local copies, waits for them, and re-layouts: 113 us -> none  [the longest x1 45.8 us: local_block(): pre_grad = act_vjp(act_grad)[0].astype(jnp.bfloat16)]
  transfers between devices with their start and end apart: 3 -> 14, of which waited for: 1 -> 6; matrix products, arithmetic and copies ran while one was open for 18% -> 4% of each run, Pallas kernels for 0% -> 59%
where the time goes in v1:
time: 1500 us; the launch traced here: 1490 us
  Pallas kernels  873 us (58%)
  waiting for transfers between devices  479 us (32%)
  other arithmetic  44.6 us (3%)
  matrix products  39.9 us (3%)
  between operations  15.5 us (1%)
    pallas_call x4, Pallas kernels, run_experts(): pl.pallas_call(functools.partial(expert_kernel, min(TILE, tokens), lane0,...  873 us
    ppermute x6, waiting for transfers between devices, exchange(): return lax.ppermute(a, 'ep', swap)  381 us
    all_gather x2, waiting for transfers between devices, gather(): return lax.all_gather(a, 'ep', axis=0, tiled=True, axis_index_groups=groups)  82.1 us
  transfers between devices with their start and end apart: 14, of which 6 were waited for; matrix products, arithmetic and copies ran while one was open for 4% of the time, Pallas kernels for 59%

profile of v1, /device:TPU:2, one launch (start us, length us, event | category | flops | bytes accessed | tf_op | source)
XLA Modules:
  0.0 1485.9 jit_solution(7693293661299419468)
XLA Ops:
  7.3 1.9 slice_bitcast_fusion.8
  9.2 0.9 copy-done.64
  10.1 2.4 convert_bitcast_fusion
  12.5 2.0 pad_maximum_fusion.3
  14.6 4.0 convert_bitcast_fusion.1
  18.6 2.0 pad_maximum_fusion.2
  20.7 1.6 collective-permute-start
  23.2 7.0 select_reduce_fusion
  30.2 3.7 fusion.22
  34.5 5.0 broadcast_select_fusion
  39.9 1.1 pad.12
  41.0 0.7 collective-permute-start.2
  41.7 1.4 collective-permute-start.1
  43.8 1.0 pad.11.refs_2_
  44.8 10.1 all_gather.10
  54.9 0.7 slice_bitcast_fusion.11
  55.6 82.1 %all-gather.7.cloned.1.call-done = bf16[12288,1024]{1,0:T(8,128)(2,1)} async-done(((bf16[1536,1024]{1,0:T(8,128)(2,1)}), bf16[12288,1024]{1,0:T(8,128)(2,1)}) %all-gather.7.cloned.1.call-update) | async-done | bytes 25165840 | tf_op jit(solution)/shard_map/all_gather | solution.py:139
  137.6 210.6 %experts.4 = (f32[2048,1024]{1,0:T(8,128)}, f32[2048,1024]{1,0:T(8,128)}, f32[2048,128]{1,0:T(8,128)}, f32[8,1544,1024]{2,1,0:T(8,128)}) custom-call(bf16[2048,1024]{1,0:T(8,128)(2,1)} %refs_0_.3, bf16[2048,1024]{1,0:T(8,128)(2,1)} %refs_1_.3, f32[2048,128]{1,0:T(8,128)} %pad.11.refs_2_, bf16[8,1536,1024]{2,1,0:T(8,128)(2,1)} %bitcast.136, ...), custom_call_target="tpu_custom_call" | custom-call | flops 154618822656 | bytes 117702656 | tf_op jit(solution)/shard_map/experts/pallas_call | solution.py:123
  348.3 212.2 %experts.5 = (f32[2048,1024]{1,0:T(8,128)}, f32[2048,1024]{1,0:T(8,128)}, f32[2048,128]{1,0:T(8,128)}, f32[8,1544,1024]{2,1,0:T(8,128)}) custom-call(bf16[2048,1024]{1,0:T(8,128)(2,1)} %collective-permute-done.refs_0_, bf16[2048,1024]{1,0:T(8,128)(2,1)} %collective-permute-done.1.refs_1_, f32[2048,128]{1,0:T(8,128)} %collective-permute-done.2.refs_2_, ...), custom_call_target="tpu_custom_call" | custom-call | flops 154618822656 | bytes 117702656 | tf_op jit(solution)/shard_map/experts/pallas_call | solution.py:123
  560.6 232.1 %experts.6 = (f32[2048,1024]{1,0:T(8,128)}, f32[2048,1024]{1,0:T(8,128)}, f32[2048,128]{1,0:T(8,128)}, f32[8,1544,1024]{2,1,0:T(8,128)}) custom-call(bf16[2048,1024]{1,0:T(8,128)(2,1)} %collective-permute-done.refs_0_, bf16[2048,1024]{1,0:T(8,128)(2,1)} %collective-permute-done.1.refs_1_, f32[2048,128]{1,0:T(8,128)} %collective-permute-done.2.refs_2_, ...), custom_call_target="tpu_custom_call" | custom-call | flops 154618822656 | bytes 117702656 | tf_op jit(solution)/shard_map/experts/pallas_call | solution.py:123
  792.7 218.3 %experts.7 = (f32[2048,1024]{1,0:T(8,128)}, f32[2048,1024]{1,0:T(8,128)}, f32[2048,128]{1,0:T(8,128)}, f32[8,1544,1024]{2,1,0:T(8,128)}) custom-call(bf16[2048,1024]{1,0:T(8,128)(2,1)} %refs_0_.3, bf16[2048,1024]{1,0:T(8,128)(2,1)} %refs_1_.3, f32[2048,128]{1,0:T(8,128)} %pad.11.refs_2_, bf16[8,1536,1024]{2,1,0:T(8,128)(2,1)} %bitcast.135, ...), custom_call_target="tpu_custom_call" | custom-call | flops 154618822656 | bytes 117702656 | tf_op jit(solution)/shard_map/experts/pallas_call | solution.py:123
  1011.1 1.5 collective-permute-start.4
  1013.4 1.5 collective-permute-start.5
  1014.9 381.0 %collective-permute-done.5 = f32[2048,128]{1,0:T(8,128)S(1)} collective-permute-done((f32[2048,128]{1,0:T(8,128)S(1)}, f32[2048,128]{1,0:T(8,128)S(1)}, u32[]{:S(2)}, u32[]{:S(2)}) %collective-permute-start.5) | collective-permute-done | bytes 1048608 | tf_op jit(solution)/shard_map/ppermute | solution.py:145
  1396.0 1.5 slice_select_fusion.1
  1397.6 6.4 multiply_reduce_fusion
  1404.1 6.2 convert_reduce_fusion
  1410.3 0.9 fusion.31
  1411.2 1.4 collective-permute-done.6
  1413.2 5.7 collective-permute-done.7
  1418.9 0.6 collective-permute-start.8
  1419.6 4.8 collective-permute-done.8
  1424.4 1.5 collective-permute-start.9
  1425.9 3.9 collective-permute-done.9
  1429.9 0.7 reshape.170
  1430.8 0.6 reshape.171
  1431.5 9.2 add_convert_fusion
  1440.7 9.3 add_convert_fusion.1
  1450.1 0.8 slice_bitcast_fusion.14
  1451.3 0.8 slice_bitcast_fusion.13
  1452.5 0.6 pad_maximum_fusion.6
  1453.1 0.6 pad_maximum_fusion.5
  1453.8 9.4 fusion.2
  1463.2 7.0 fusion.3
  1470.2 4.2 pad_maximum_fusion
  1474.4 1.6 slice-done
  1476.0 0.6 slice-done.3
  1476.7 2.3 pad_maximum_fusion.1
  (190 shorter events, 5.1 us)
Async XLA Ops:
  7.2 130.5 %all-gather.7.cloned.1.call-start = ((), (), s32[]{:S(2)}) async-start(), calls=%async_computation.5 | async-start | bytes 28311552 | tf_op jit(solution)/shard_map/all_gather | solution.py:139
  14.5 546.1 %all-gather.5.cloned.1.call-start = ((), (), s32[]{:S(2)}) async-start(), calls=%async_computation.4 | async-start | bytes 28311552 | tf_op jit(solution)/shard_map/all_gather | solution.py:139
  20.6 1429.4 %reduce-scatter.3.cloned.1.call-start = ((), (), s32[]{:S(2)}) async-start(), calls=%async_computation.2 | async-start | bytes 56918016 | tf_op jit(solution)/shard_map/reduce_scatter | solution.py:142
  20.7 327.6 %collective-permute-start = (bf16[2048,1024]{1,0:T(8,128)(2,1)}, bf16[2048,1024]{1,0:T(8,128)(2,1)}, u32[]{:S(2)}, u32[]{:S(2)}) collective-permute-start(bf16[2048,1024]{1,0:T(8,128)(2,1)} %refs_0_.3), channel_id=1, source_target_pairs={{0,8},{1,9},{2,10},{3,11},{4,12},{5,13},{6,14},{7,15},{8,0},{9,1},... | collective-permute-start | bytes 12582920 | tf_op jit(solution)/shard_map/ppermute | solution.py:145
  22.4 11.6 copy-start.47
  23.0 11.0 copy-start.31
  23.0 11.0 copy-start.33
  23.0 11.0 copy-start.35
  23.0 11.0 copy-start.37
  41.0 307.3 %collective-permute-start.2 = (f32[2048,128]{1,0:T(8,128)}, f32[2048,128]{1,0:T(8,128)}, u32[]{:S(2)}, u32[]{:S(2)}) collective-permute-start(f32[2048,128]{1,0:T(8,128)} %pad.12), channel_id=1, source_target_pairs={{0,8},{1,9},{2,10},{3,11},{4,12},{5,13},{6,14},{7,15},{8,0},{9,1},... | collective-permute-start | bytes 3145736 | tf_op jit(solution)/shard_map/ppermute | solution.py:145
  41.7 306.6 %collective-permute-start.1 = (bf16[2048,1024]{1,0:T(8,128)(2,1)}, bf16[2048,1024]{1,0:T(8,128)(2,1)}, u32[]{:S(2)}, u32[]{:S(2)}) collective-permute-start(bf16[2048,1024]{1,0:T(8,128)(2,1)} %refs_1_.3), channel_id=1, source_target_pairs={{0,8},{1,9},{2,10},{3,11},{4,12},{5,13},{6,14},{7,15},{8,0},{9,1},... | collective-permute-start | bytes 12582920 | tf_op jit(solution)/shard_map/ppermute | solution.py:145
  560.5 890.8 %reduce-scatter.5.cloned.1.call-start = ((), (), s32[]{:S(2)}) async-start(), calls=%async_computation.3 | async-start | bytes 56918016 | tf_op jit(solution)/shard_map/reduce_scatter | solution.py:142
  1011.0 385.0 %copy-start.5 = (f32[2048,128]{1,0:T(8,128)S(1)}, f32[2048,128]{1,0:T(8,128)}, u32[]{:S(2)}) copy-start(f32[2048,128]{1,0:T(8,128)} %get-tuple-element.36) | copy-start | bytes 3145732
  1011.1 420.4 %collective-permute-start.4 = (f32[2048,1024]{1,0:T(8,128)}, f32[2048,1024]{1,0:T(8,128)}, u32[]{:S(2)}, u32[]{:S(2)}) collective-permute-start(f32[2048,1024]{1,0:T(8,128)} %get-tuple-element.33), channel_id=1, source_target_pairs={{0,8},{1,9},{2,10},{3,11},{4,12},{5,13},{6,14},{7,15},{8,0},{9,1},... | collective-permute-start | bytes 25165832 | tf_op jit(solution)/shard_map/ppermute | solution.py:145
  1012.6 428.1 %collective-permute-start.3 = (f32[2048,1024]{1,0:T(8,128)}, f32[2048,1024]{1,0:T(8,128)}, u32[]{:S(2)}, u32[]{:S(2)}) collective-permute-start(f32[2048,1024]{1,0:T(8,128)} %get-tuple-element.31), channel_id=1, source_target_pairs={{0,8},{1,9},{2,10},{3,11},{4,12},{5,13},{6,14},{7,15},{8,0},{9,1},... | collective-permute-start | bytes 25165832 | tf_op jit(solution)/shard_map/ppermute | solution.py:145
  1013.1 384.3 %copy-start.1 = (f32[2048,32]{1,0:T(8,128)S(1)}, f32[2048,32]{1,0:T(8,128)}, u32[]{:S(2)}) copy-start(f32[2048,32]{1,0:T(8,128)} %copy-done) | copy-start | bytes 786436
  1013.1 384.3 %copy-start.9 = (s32[2048,1]{0,1:T(1,128)S(1)}, s32[2048,1]{0,1:T(1,128)}, u32[]{:S(2)}) copy-start(s32[2048,1]{0,1:T(1,128)} %copy-done.8) | copy-start | bytes 24580
  1013.1 384.3 %copy-start.11 = (s32[2048,1]{0,1:T(1,128)S(1)}, s32[2048,1]{0,1:T(1,128)}, u32[]{:S(2)}) copy-start(s32[2048,1]{0,1:T(1,128)} %copy-done.10) | copy-start | bytes 24580
  1013.1 384.3 %copy-start.13 = (s32[2048,1]{0,1:T(1,128)S(1)}, s32[2048,1]{0,1:T(1,128)}, u32[]{:S(2)}) copy-start(s32[2048,1]{0,1:T(1,128)} %copy-done.12) | copy-start | bytes 24580
  1013.2 384.3 %copy-start.15 = (s32[2048,1]{0,1:T(1,128)S(1)}, s32[2048,1]{0,1:T(1,128)}, u32[]{:S(2)}) copy-start(s32[2048,1]{0,1:T(1,128)} %copy-done.14) | copy-start | bytes 24580
  1013.2 384.3 %copy-start.17 = (s32[2048,1]{0,1:T(1,128)S(1)}, s32[2048,1]{0,1:T(1,128)}, u32[]{:S(2)}) copy-start(s32[2048,1]{0,1:T(1,128)} %copy-done.16) | copy-start | bytes 24580
  1013.2 384.3 %copy-start.19 = (s32[2048,1]{0,1:T(1,128)S(1)}, s32[2048,1]{0,1:T(1,128)}, u32[]{:S(2)}) copy-start(s32[2048,1]{0,1:T(1,128)} %copy-done.18) | copy-start | bytes 24580
  1013.2 384.3 %copy-start.21 = (s32[2048,1]{0,1:T(1,128)S(1)}, s32[2048,1]{0,1:T(1,128)}, u32[]{:S(2)}) copy-start(s32[2048,1]{0,1:T(1,128)} %copy-done.20) | copy-start | bytes 24580
  1013.2 384.3 %copy-start.23 = (s32[2048,1]{0,1:T(1,128)S(1)}, s32[2048,1]{0,1:T(1,128)}, u32[]{:S(2)}) copy-start(s32[2048,1]{0,1:T(1,128)} %copy-done.22) | copy-start | bytes 24580
  1013.2 384.3 %copy-start.25 = (f32[2048]{0:T(1024)S(1)}, f32[2048]{0:T(1024)}, u32[]{:S(2)}) copy-start(f32[2048]{0:T(1024)} %copy-done.24) | copy-start | bytes 24580
  1013.2 384.3 %copy-start.27 = (f32[2048]{0:T(1024)S(1)}, f32[2048]{0:T(1024)}, u32[]{:S(2)}) copy-start(f32[2048]{0:T(1024)} %copy-done.26) | copy-start | bytes 24580
  1013.2 384.3 %copy-start.32 = (pred[2048]{0:T(1024)(128)(4,1)S(1)}, pred[2048]{0:T(1024)(128)(4,1)}, u32[]{:S(2)}) copy-start(pred[2048]{0:T(1024)(128)(4,1)} %copy-done.31) | copy-start | bytes 6148
  1013.2 384.3 %copy-start.34 = (pred[2048]{0:T(1024)(128)(4,1)S(1)}, pred[2048]{0:T(1024)(128)(4,1)}, u32[]{:S(2)}) copy-start(pred[2048]{0:T(1024)(128)(4,1)} %copy-done.33) | copy-start | bytes 6148
  1013.3 384.3 %copy-start.36 = (pred[2048]{0:T(1024)(128)(4,1)S(1)}, pred[2048]{0:T(1024)(128)(4,1)}, u32[]{:S(2)}) copy-start(pred[2048]{0:T(1024)(128)(4,1)} %copy-done.35) | copy-start | bytes 6148
  1013.3 384.3 %copy-start.38 = (pred[2048]{0:T(1024)(128)(4,1)S(1)}, pred[2048]{0:T(1024)(128)(4,1)}, u32[]{:S(2)}) copy-start(pred[2048]{0:T(1024)(128)(4,1)} %copy-done.37) | copy-start | bytes 6148
  1013.3 384.3 %copy-start.40 = (pred[2048]{0:T(1024)(128)(4,1)S(1)}, pred[2048]{0:T(1024)(128)(4,1)}, u32[]{:S(2)}) copy-start(pred[2048]{0:T(1024)(128)(4,1)} %copy-done.39) | copy-start | bytes 6148
  1013.3 384.3 %copy-start.42 = (pred[2048]{0:T(1024)(128)(4,1)S(1)}, pred[2048]{0:T(1024)(128)(4,1)}, u32[]{:S(2)}) copy-start(pred[2048]{0:T(1024)(128)(4,1)} %copy-done.41) | copy-start | bytes 6148
  1013.3 384.3 %copy-start.44 = (pred[2048]{0:T(1024)(128)(4,1)S(1)}, pred[2048]{0:T(1024)(128)(4,1)}, u32[]{:S(2)}) copy-start(pred[2048]{0:T(1024)(128)(4,1)} %copy-done.43) | copy-start | bytes 6148
  1013.3 384.3 %copy-start.46 = (pred[2048]{0:T(1024)(128)(4,1)S(1)}, pred[2048]{0:T(1024)(128)(4,1)}, u32[]{:S(2)}) copy-start(pred[2048]{0:T(1024)(128)(4,1)} %copy-done.45) | copy-start | bytes 6148
  1013.3 384.3 %copy-start.48 = (s32[32]{0:T(128)S(1)}, s32[32]{0:T(128)}, u32[]{:S(2)}) copy-start(s32[32]{0:T(128)} %copy-done.47) | copy-start | bytes 388
  1013.4 382.5 %collective-permute-start.5 = (f32[2048,128]{1,0:T(8,128)S(1)}, f32[2048,128]{1,0:T(8,128)S(1)}, u32[]{:S(2)}, u32[]{:S(2)}) collective-permute-start(f32[2048,128]{1,0:T(8,128)S(1)} %add.92), channel_id=1, source_target_pairs={{0,8},{1,9},{2,10},{3,11},{4,12},{5,13},{6,14},{7,15},{8,0},{9,1},... | collective-permute-start | bytes 3145736 | tf_op jit(solution)/shard_map/ppermute | solution.py:145
  1397.4 12.8 copy-start.2
  1410.3 21.2 %copy-start.7 = (bf16[1024,2,2,8]{0,3,2,1:T(8,128)(2,1)S(1)}, bf16[1024,2,2,8]{0,3,2,1:T(8,128)(2,1)}, u32[]{:S(2)}) copy-start(bf16[1024,2,2,8]{0,3,2,1:T(8,128)(2,1)} %copy-done.6) | copy-start | bytes 196612
  1411.2 1.4 collective-permute-start.6
  1412.6 6.3 collective-permute-start.7
  1418.9 5.4 collective-permute-start.8
  1424.4 5.4 collective-permute-start.9
  1440.7 13.1 copy-start.52
  1440.7 13.1 copy-start.54
  1440.7 13.1 copy-start.56
  1440.7 13.1 copy-start.58
  1440.7 13.0 copy-start.60
  1440.7 13.0 copy-start.62
  (35 other events, 250.9 us)
Sparse Core Ops, SparseCore 0:
  14.6 123.0 all-gather.6
  140.1 121.4 all-gather.4
  560.6 279.9 reduce-scatter.2
  1011.2 280.0 reduce-scatter.4

commit v2 on v1

--- a/solution.py
+++ b/solution.py
@@ -17,7 +17,7 @@
     return lax.dot_general(a, b, (((ca,), (cb,)), ((), ())), preferred_element_type=F32)
 
 
-def expert_kernel(tile, lane0, has_acc, has_grad, *refs):
+def expert_kernel(tile, lane0, stride, first, has_acc, has_grad, *refs):
     it = iter(refs)
     x_ref, dy_ref, gate_ref, w_ref, b_ref = (next(it) for _ in range(5))
     acc_refs = [next(it) for _ in range(2)] if has_acc else []
@@ -37,7 +37,7 @@
                 load.start()
         r_ref[...] = jnp.zeros_like(r_ref)
         if has_grad:
-            pltpu.make_async_copy(gin_ref.at[0], gbuf_ref, grad_sem).start()
+            pltpu.make_async_copy(gin_ref.at[first], gbuf_ref, grad_sem).start()
         if has_acc:
             for load in loads:
                 load.wait()
@@ -46,12 +46,12 @@
             dx_ref[...] = jnp.zeros_like(dx_ref)
 
     if has_grad:
-        pltpu.make_async_copy(gin_ref.at[expert], gbuf_ref, grad_sem).wait()
+        pltpu.make_async_copy(gin_ref.at[first + stride * expert], gbuf_ref, grad_sem).wait()
         grad_ref[0] = gbuf_ref[...]
 
         @pl.when(expert + 1 < pl.num_programs(0))
         def _():
-            pltpu.make_async_copy(gin_ref.at[expert + 1], gbuf_ref, grad_sem).start()
+            pltpu.make_async_copy(gin_ref.at[first + stride * (expert + 1)], gbuf_ref, grad_sem).start()
     else:
         grad_ref[...] = jnp.zeros_like(grad_ref)
 
@@ -61,12 +61,12 @@
         dy = dy_ref[rows, :]
         gates = gate_ref[rows, :]
         lane = lax.broadcasted_iota(jnp.int32, gates.shape, 1)
-        here = lane == expert + lane0
+        here = lane == lane0 + first + stride * expert
         w = jnp.sum(jnp.where(here, gates, 0.0), axis=1, keepdims=True)
         dyf = dy.astype(F32)
         q = (w * dyf).astype(BF16)
-        hg = dot(x, w_ref[0, :d_model, :ff], 1, 0) + b_ref[0, 0:1, :ff]
-        hu = dot(x, w_ref[0, :d_model, ff:], 1, 0) + b_ref[0, 0:1, ff:]
+        h = dot(x, w_ref[0, :d_model, :], 1, 0) + b_ref[0, 0:1, :]
+        hg, hu = h[:, :ff], h[:, ff:]
         g = jnp.minimum(hg, SWIGLU_LIMIT)
         u = jnp.clip(hu, -SWIGLU_LIMIT, SWIGLU_LIMIT)
         u1 = u + 1.0
@@ -83,30 +83,30 @@
         u_pass = jnp.where(mag < SWIGLU_LIMIT, 1.0, jnp.where(mag == SWIGLU_LIMIT, 0.5, 0.0))
         dg = (da * u1 * (s + SWIGLU_ALPHA * gs * (1.0 - s)) * g_pass).astype(BF16)
         du = (da * gs * u_pass).astype(BF16)
-        p = dot(dg, w_ref[0, :d_model, :ff], 1, 1) + dot(du, w_ref[0, :d_model, ff:], 1, 1)
+        dh = jnp.concatenate([dg, du], axis=1)
+        p = dot(dh, w_ref[0, :d_model, :], 1, 1)
         dx_ref[rows, :] += p.astype(BF16).astype(F32)
-        grad_ref[0, :d_model, :ff] += dot(x, dg, 0, 0)
-        grad_ref[0, :d_model, ff:] += dot(x, du, 0, 0)
+        grad_ref[0, :d_model, :] += dot(x, dh, 0, 0)
         grad_ref[0, d_model:d_model + ff, :] += dot(act, q, 0, 0)
         row = d_model + ff
-        grad_ref[0, row:row + 1, :ff] += jnp.sum(dg.astype(F32), axis=0, keepdims=True)
-        grad_ref[0, row:row + 1, ff:] += jnp.sum(du.astype(F32), axis=0, keepdims=True)
+        grad_ref[0, row:row + 1, :] += jnp.sum(dh.astype(F32), axis=0, keepdims=True)
         grad_ref[0, row + 1:row + 2, :] += jnp.sum(q.astype(F32), axis=0, keepdims=True)
         return carry
 
     lax.fori_loop(0, tokens // tile, body, 0)
 
 
-def run_experts(lane0, x, dy, gates, weights, bias, acc=None, grad_in=None):
+def run_experts(lane0, x, dy, gates, weights, bias, acc=None, grad_in=None, stride=1, first=0):
     tokens, d_model = x.shape
-    experts, w_rows, _ = weights.shape
-    g_rows = w_rows + 8
+    experts, w_rows = weights.shape[0] // stride, weights.shape[1]
+    g_rows = w_rows + 16
     once = lambda e: (0, 0)
     per = lambda e: (e, 0, 0)
+    pick = lambda e: (first + stride * e, 0, 0)
     keep = pl.Buffered(1)
     full = lambda a: pl.BlockSpec(a.shape, once, pipeline_mode=keep)
     args = [x, dy, gates, weights, bias]
-    specs = [full(x), full(dy), full(gates), pl.BlockSpec((1, w_rows, d_model), per), pl.BlockSpec((1, 2, d_model), per)]
+    specs = [full(x), full(dy), full(gates), pl.BlockSpec((1, w_rows, d_model), pick), pl.BlockSpec((1, 2, d_model), pick)]
     scratch = []
     if acc is not None:
         args += list(acc)
@@ -121,7 +121,7 @@
     out_specs = [pl.BlockSpec((tokens, d_model), once, pipeline_mode=keep)] * 2 + [pl.BlockSpec(gates.shape, once, pipeline_mode=keep), pl.BlockSpec((1, g_rows, d_model), per)]
     flops = 2 * experts * tokens * d_model * d_model * 9 // 2
     return pl.pallas_call(
-        functools.partial(expert_kernel, min(TILE, tokens), lane0, acc is not None, grad_in is not None),
+        functools.partial(expert_kernel, min(TILE, tokens), lane0, stride, first, acc is not None, grad_in is not None),
         grid=(experts,), in_specs=specs, out_specs=out_specs, out_shape=out_shape, scratch_shapes=scratch,
         compiler_params=pltpu.CompilerParams(dimension_semantics=("arbitrary",), vmem_limit_bytes=67043328),
         cost_estimate=pl.CostEstimate(flops=flops, bytes_accessed=experts * (w_rows * 2 + g_rows * 4) * d_model + tokens * d_model * 20, transcendentals=0),
@@ -194,17 +194,22 @@
         r_far = exchange(r_2 + r_3)
         dx_far = exchange(dx_3)
         out_far = exchange(out_3)
-        out_4, dx_4, r_4, gr_b = run_experts(group, hidden, grad_out, g_own, w_all[1], b_all[:, 1], acc=(out_1, dx_1), grad_in=gr_3)
-        part_b = scatter(gr_b)
-
-        block_out = (out_4 + out_far).astype(BF16)
-        r_own = (r_1 + r_4)[:, :half]
+        out_4, dx_4, r_4, gr_b = run_experts(group, hidden, grad_out, g_own, w_all[1], b_all[:, 1], acc=(out_1, dx_1), grad_in=gr_3, stride=2, first=0)
+        half_0 = scatter(gr_b.reshape(-1, d_model))
+        out_5, dx_5, r_5, gr_c = run_experts(group, hidden, grad_out, g_own, w_all[1], b_all[:, 1], acc=(out_4, dx_4), grad_in=gr_3, stride=2, first=1)
+        half_1 = scatter(gr_c.reshape(-1, d_model))
+        odd = lax.axis_index('ep') % 2 == 1
+        got = lax.ppermute(jnp.where(odd, half_0, half_1), 'ep', [(i, i ^ 1) for i in range(ep_size)])
+        part_b = jnp.concatenate([jnp.where(odd, got, half_0), jnp.where(odd, half_1, got)], axis=0)[None]
+
+        block_out = (out_5 + out_far).astype(BF16)
+        r_own = (r_1 + r_4 + r_5)[:, :half]
         r_oth = r_far[:, :half]
         gate_grad = jnp.where(kept, jnp.concatenate([jnp.where(upper, r_oth, r_own), jnp.where(upper, r_own, r_oth)], axis=1), 0.0)
         sel_grad = gate * (gate_grad - jnp.sum(gate * gate_grad, axis=1, keepdims=True))
         logit_grad = sel_grad.astype(BF16)
         router_dx = jnp.einsum('te,de->td', logit_grad, w_rt, preferred_element_type=F32)
-        grad_hidden = (dx_4 + dx_far + router_dx).astype(BF16)
+        grad_hidden = (dx_5 + dx_far + router_dx).astype(BF16)
         grad_rt = jnp.concatenate([jnp.einsum('te,td->ed', logit_grad, hidden, preferred_element_type=F32), jnp.pad(jnp.sum(logit_grad, axis=0, dtype=F32)[None], ((0, 7), (0, d_model - experts)))], axis=0)
         step = 1
         while step < ep_size:

time: 1500 us -> 1660 us (1.11)
  waiting for transfers between devices: 479 us -> 608 us
    reduce_scatter x2 -> x3, waiting for transfers between devices: 0.02 us -> 119 us  [scatter(): lax.psum_scatter(a, 'ep', scatter_dimension=0, tiled=True, axis_index_gro...]
    pallas_call x4 -> x5, Pallas kernels: 873 us -> 888 us  [run_experts(): pl.pallas_call(functools.partial(expert_kernel, min(TILE, tokens), lane0,...]
  transfers between devices with their start and end apart: 14 -> 16, of which waited for: 6 -> 7; matrix products, arithmetic and copies ran while one was open for 4% -> 5% of each run, Pallas kernels for 59% -> 26%
where the time goes in v2:
time: 1660 us; the launch traced here: 1650 us
  Pallas kernels  888 us (53%)
  waiting for transfers between devices  608 us (37%)
  other arithmetic  58.5 us (4%)
  matrix products  43.3 us (3%)
    pallas_call x5, Pallas kernels, run_experts(): pl.pallas_call(functools.partial(expert_kernel, min(TILE, tokens), lane0,...  888 us
    ppermute x6, waiting for transfers between devices, exchange(): return lax.ppermute(a, 'ep', swap)  378 us
    reduce_scatter x3, waiting for transfers between devices, scatter(): lax.psum_scatter(a, 'ep', scatter_dimension=0, tiled=True, axis_index_gro...  119 us
    all_gather x2, waiting for transfers between devices, gather(): return lax.all_gather(a, 'ep', axis=0, tiled=True, axis_index_groups=groups)  82.1 us
  transfers between devices with their start and end apart: 16, of which 7 were waited for; matrix products, arithmetic and copies ran while one was open for 5% of the time, Pallas kernels for 26%

profile of v2, /device:TPU:2, one launch (start us, length us, event | category | flops | bytes accessed | tf_op | source)
XLA Modules:
  0.0 1648.8 jit_solution(16326999163270716632)
XLA Ops:
  7.3 1.9 slice_bitcast_fusion.8
  9.2 0.9 copy-done.67
  10.1 2.4 convert_bitcast_fusion
  12.5 2.0 pad_maximum_fusion.3
  14.6 4.0 convert_bitcast_fusion.1
  18.6 2.0 pad_maximum_fusion.2
  20.7 1.6 collective-permute-start
  23.2 7.0 select_reduce_fusion
  30.2 3.7 fusion.22
  34.5 5.0 broadcast_select_fusion.3
  39.9 1.1 pad.12
  41.0 0.7 collective-permute-start.2
  41.6 1.4 collective-permute-start.1
  43.7 1.0 pad.11.refs_2_
  44.8 10.1 all_gather.10
  55.5 82.1 %all-gather.7.cloned.1.call-done = bf16[12288,1024]{1,0:T(8,128)(2,1)} async-done(((bf16[1536,1024]{1,0:T(8,128)(2,1)}), bf16[12288,1024]{1,0:T(8,128)(2,1)}) %all-gather.7.cloned.1.call-update) | async-done | bytes 25165840 | tf_op jit(solution)/shard_map/all_gather | solution.py:139
  137.6 211.3 %experts.5 = (f32[2048,1024]{1,0:T(8,128)}, f32[2048,1024]{1,0:T(8,128)}, f32[2048,128]{1,0:T(8,128)}, f32[8,1552,1024]{2,1,0:T(8,128)}) custom-call(bf16[2048,1024]{1,0:T(8,128)(2,1)} %refs_0_.5, bf16[2048,1024]{1,0:T(8,128)(2,1)} %refs_1_.5, f32[2048,128]{1,0:T(8,128)} %pad.11.refs_2_, bf16[8,1536,1024]{2,1,0:T(8,128)(2,1)} %bitcast.141, ...), custom_call_target="tpu_custom_call" | custom-call | flops 154618822656 | bytes 117964800 | tf_op jit(solution)/shard_map/experts/pallas_call | solution.py:123
  349.0 213.0 %experts.6 = (f32[2048,1024]{1,0:T(8,128)}, f32[2048,1024]{1,0:T(8,128)}, f32[2048,128]{1,0:T(8,128)}, f32[8,1552,1024]{2,1,0:T(8,128)}) custom-call(bf16[2048,1024]{1,0:T(8,128)(2,1)} %collective-permute-done.refs_0_, bf16[2048,1024]{1,0:T(8,128)(2,1)} %collective-permute-done.1.refs_1_, f32[2048,128]{1,0:T(8,128)} %collective-permute-done.2.refs_2_, ...), custom_call_target="tpu_custom_call" | custom-call | flops 154618822656 | bytes 117964800 | tf_op jit(solution)/shard_map/experts/pallas_call | solution.py:123
  562.1 224.8 %experts.7 = (f32[2048,1024]{1,0:T(8,128)}, f32[2048,1024]{1,0:T(8,128)}, f32[2048,128]{1,0:T(8,128)}, f32[8,1552,1024]{2,1,0:T(8,128)}) custom-call(bf16[2048,1024]{1,0:T(8,128)(2,1)} %collective-permute-done.refs_0_, bf16[2048,1024]{1,0:T(8,128)(2,1)} %collective-permute-done.1.refs_1_, f32[2048,128]{1,0:T(8,128)} %collective-permute-done.2.refs_2_, ...), custom_call_target="tpu_custom_call" | custom-call | flops 154618822656 | bytes 117964800 | tf_op jit(solution)/shard_map/experts/pallas_call | solution.py:123
  786.9 119.3 %experts.8 = (f32[2048,1024]{1,0:T(8,128)}, f32[2048,1024]{1,0:T(8,128)}, f32[2048,128]{1,0:T(8,128)}, f32[4,1552,1024]{2,1,0:T(8,128)}) custom-call(bf16[2048,1024]{1,0:T(8,128)(2,1)} %refs_0_.5, bf16[2048,1024]{1,0:T(8,128)(2,1)} %refs_1_.5, f32[2048,128]{1,0:T(8,128)} %pad.11.refs_2_, bf16[8,1536,1024]{2,1,0:T(8,128)(2,1)} %bitcast.139, ...), custom_call_target="tpu_custom_call" | custom-call | flops 77309411328 | bytes 79953920 | tf_op jit(solution)/shard_map/experts/pallas_call | solution.py:123
  906.2 119.5 %experts.9 = (f32[2048,1024]{1,0:T(8,128)}, f32[2048,1024]{1,0:T(8,128)}, f32[2048,128]{1,0:T(8,128)}, f32[4,1552,1024]{2,1,0:T(8,128)}) custom-call(bf16[2048,1024]{1,0:T(8,128)(2,1)} %refs_0_.5, bf16[2048,1024]{1,0:T(8,128)(2,1)} %refs_1_.5, f32[2048,128]{1,0:T(8,128)} %pad.11.refs_2_, bf16[8,1536,1024]{2,1,0:T(8,128)(2,1)} %bitcast.140, ...), custom_call_target="tpu_custom_call" | custom-call | flops 77309411328 | bytes 79953920 | tf_op jit(solution)/shard_map/experts/pallas_call | solution.py:123
  1026.9 1.5 collective-permute-start.4
  1029.1 3.6 add.101
  1032.8 1.5 collective-permute-start.5
  1034.2 377.9 %collective-permute-done.5 = f32[2048,128]{1,0:T(8,128)} collective-permute-done((f32[2048,128]{1,0:T(8,128)}, f32[2048,128]{1,0:T(8,128)}, u32[]{:S(2)}, u32[]{:S(2)}) %collective-permute-start.5) | collective-permute-done | bytes 1048608 | tf_op jit(solution)/shard_map/ppermute | solution.py:145
  1412.1 1.8 slice_select_fusion.1
  1414.1 6.4 multiply_reduce_fusion
  1420.5 6.2 convert_reduce_fusion
  1426.8 5.0 broadcast_select_fusion.2
  1431.8 0.9 fusion.31
  1433.2 4.7 collective-permute-done.6
  1438.6 9.8 collective-permute-done.7
  1449.0 9.6 collective-permute-done.8
  1458.6 1.5 collective-permute-start.9
  1460.1 3.9 collective-permute-done.9
  1464.1 0.7 reshape.176
  1465.6 9.4 add_convert_fusion
  1475.1 9.9 add_convert_fusion.1
  1485.0 3.3 broadcast_select_fusion.1
  1488.3 1.1 maximum_bitcast_fusion
  1489.5 2.5 copy-done.4
  1492.5 10.3 fusion.3
  1502.7 118.5 %reduce-scatter.4.cloned.1.call-done = f32[1,1552,1024]{2,1,0:T(8,128)} async-done(((f32[8,1552,1024]{2,1,0:T(8,128)}), f32[1,1552,1024]{2,1,0:T(8,128)}) %reduce-scatter.4.cloned.1.call-update) | async-done | bytes 6357008 | tf_op jit(solution)/shard_map/reduce_scatter | solution.py:142
  1621.2 0.8 slice_bitcast_fusion.14
  1623.6 9.4 fusion.2
  1633.0 4.2 pad_maximum_fusion
  1637.3 1.6 slice-done
  1639.5 2.3 pad_maximum_fusion.1
  (200 shorter events, 10.3 us)
Async XLA Ops:
  7.2 130.5 %all-gather.7.cloned.1.call-start = ((), (), s32[]{:S(2)}) async-start(), calls=%async_computation.7 | async-start | bytes 28311552 | tf_op jit(solution)/shard_map/all_gather | solution.py:139
  14.5 547.6 %all-gather.5.cloned.1.call-start = ((), (), s32[]{:S(2)}) async-start(), calls=%async_computation.6 | async-start | bytes 28311552 | tf_op jit(solution)/shard_map/all_gather | solution.py:139
  20.6 1406.1 %reduce-scatter.8.cloned.1.call-start = ((), (), s32[]{:S(2)}) async-start(), calls=%async_computation.5 | async-start | bytes 28606464 | tf_op jit(solution)/shard_map/reduce_scatter | solution.py:142
  20.7 328.3 %collective-permute-start = (bf16[2048,1024]{1,0:T(8,128)(2,1)}, bf16[2048,1024]{1,0:T(8,128)(2,1)}, u32[]{:S(2)}, u32[]{:S(2)}) collective-permute-start(bf16[2048,1024]{1,0:T(8,128)(2,1)} %refs_0_.5), channel_id=1, source_target_pairs={{0,8},{1,9},{2,10},{3,11},{4,12},{5,13},{6,14},{7,15},{8,0},{9,1},... | collective-permute-start | bytes 12582920 | tf_op jit(solution)/shard_map/ppermute | solution.py:145
  22.4 11.6 copy-start.50
  23.0 11.0 copy-start.34
  23.0 11.0 copy-start.36
  23.0 11.0 copy-start.38
  23.0 11.0 copy-start.40
  23.0 11.0 copy-start.42
  23.0 11.0 copy-start.44
  23.0 11.0 copy-start.46
  23.0 11.0 copy-start.48
  41.0 308.0 %collective-permute-start.2 = (f32[2048,128]{1,0:T(8,128)}, f32[2048,128]{1,0:T(8,128)}, u32[]{:S(2)}, u32[]{:S(2)}) collective-permute-start(f32[2048,128]{1,0:T(8,128)} %pad.12), channel_id=1, source_target_pairs={{0,8},{1,9},{2,10},{3,11},{4,12},{5,13},{6,14},{7,15},{8,0},{9,1},... | collective-permute-start | bytes 3145736 | tf_op jit(solution)/shard_map/ppermute | solution.py:145
  41.6 307.4 %collective-permute-start.1 = (bf16[2048,1024]{1,0:T(8,128)(2,1)}, bf16[2048,1024]{1,0:T(8,128)(2,1)}, u32[]{:S(2)}, u32[]{:S(2)}) collective-permute-start(bf16[2048,1024]{1,0:T(8,128)(2,1)} %refs_1_.5), channel_id=1, source_target_pairs={{0,8},{1,9},{2,10},{3,11},{4,12},{5,13},{6,14},{7,15},{8,0},{9,1},... | collective-permute-start | bytes 12582920 | tf_op jit(solution)/shard_map/ppermute | solution.py:145
  1025.7 401.0 %reduce-scatter.6.cloned.1.call-start = ((), (), s32[]{:S(2)}) async-start(), calls=%async_computation.4 | async-start | bytes 28606464 | tf_op jit(solution)/shard_map/reduce_scatter | solution.py:142
  1026.3 594.9 %reduce-scatter.4.cloned.1.call-start = ((), (), s32[]{:S(2)}) async-start(), calls=%async_computation.3 | async-start | bytes 57212928 | tf_op jit(solution)/shard_map/reduce_scatter | solution.py:142
  1026.4 385.7 %copy-start.7 = (f32[2048,128]{1,0:T(8,128)S(1)}, f32[2048,128]{1,0:T(8,128)}, u32[]{:S(2)}) copy-start(f32[2048,128]{1,0:T(8,128)} %get-tuple-element.42) | copy-start | bytes 3145732
  1026.4 385.7 %copy-start.8 = (f32[2048,128]{1,0:T(8,128)S(1)}, f32[2048,128]{1,0:T(8,128)}, u32[]{:S(2)}) copy-start(f32[2048,128]{1,0:T(8,128)} %get-tuple-element.43) | copy-start | bytes 3145732
  1026.9 438.7 %collective-permute-start.4 = (f32[2048,1024]{1,0:T(8,128)}, f32[2048,1024]{1,0:T(8,128)}, u32[]{:S(2)}, u32[]{:S(2)}) collective-permute-start(f32[2048,1024]{1,0:T(8,128)} %get-tuple-element.39), channel_id=1, source_target_pairs={{0,8},{1,9},{2,10},{3,11},{4,12},{5,13},{6,14},{7,15},{8,0},{9,1},... | collective-permute-start | bytes 25165832 | tf_op jit(solution)/shard_map/ppermute | solution.py:145
  1028.4 446.7 %collective-permute-start.3 = (f32[2048,1024]{1,0:T(8,128)}, f32[2048,1024]{1,0:T(8,128)}, u32[]{:S(2)}, u32[]{:S(2)}) collective-permute-start(f32[2048,1024]{1,0:T(8,128)} %get-tuple-element.37), channel_id=1, source_target_pairs={{0,8},{1,9},{2,10},{3,11},{4,12},{5,13},{6,14},{7,15},{8,0},{9,1},... | collective-permute-start | bytes 25165832 | tf_op jit(solution)/shard_map/ppermute | solution.py:145
  1029.0 384.9 %copy-start.1 = (f32[2048,32]{1,0:T(8,128)S(1)}, f32[2048,32]{1,0:T(8,128)}, u32[]{:S(2)}) copy-start(f32[2048,32]{1,0:T(8,128)} %copy-done) | copy-start | bytes 786436
  1029.0 384.9 %copy-start.12 = (s32[2048,1]{0,1:T(1,128)S(1)}, s32[2048,1]{0,1:T(1,128)}, u32[]{:S(2)}) copy-start(s32[2048,1]{0,1:T(1,128)} %copy-done.11) | copy-start | bytes 24580
  1029.0 384.9 %copy-start.14 = (s32[2048,1]{0,1:T(1,128)S(1)}, s32[2048,1]{0,1:T(1,128)}, u32[]{:S(2)}) copy-start(s32[2048,1]{0,1:T(1,128)} %copy-done.13) | copy-start | bytes 24580
  1029.0 384.9 %copy-start.16 = (s32[2048,1]{0,1:T(1,128)S(1)}, s32[2048,1]{0,1:T(1,128)}, u32[]{:S(2)}) copy-start(s32[2048,1]{0,1:T(1,128)} %copy-done.15) | copy-start | bytes 24580
  1029.0 384.9 %copy-start.18 = (s32[2048,1]{0,1:T(1,128)S(1)}, s32[2048,1]{0,1:T(1,128)}, u32[]{:S(2)}) copy-start(s32[2048,1]{0,1:T(1,128)} %copy-done.17) | copy-start | bytes 24580
  1029.0 384.9 %copy-start.20 = (s32[2048,1]{0,1:T(1,128)S(1)}, s32[2048,1]{0,1:T(1,128)}, u32[]{:S(2)}) copy-start(s32[2048,1]{0,1:T(1,128)} %copy-done.19) | copy-start | bytes 24580
  1029.0 384.9 %copy-start.22 = (s32[2048,1]{0,1:T(1,128)S(1)}, s32[2048,1]{0,1:T(1,128)}, u32[]{:S(2)}) copy-start(s32[2048,1]{0,1:T(1,128)} %copy-done.21) | copy-start | bytes 24580
  1029.0 384.9 %copy-start.24 = (s32[2048,1]{0,1:T(1,128)S(1)}, s32[2048,1]{0,1:T(1,128)}, u32[]{:S(2)}) copy-start(s32[2048,1]{0,1:T(1,128)} %copy-done.23) | copy-start | bytes 24580
  1029.0 384.9 %copy-start.26 = (s32[2048,1]{0,1:T(1,128)S(1)}, s32[2048,1]{0,1:T(1,128)}, u32[]{:S(2)}) copy-start(s32[2048,1]{0,1:T(1,128)} %copy-done.25) | copy-start | bytes 24580
  1029.0 384.9 %copy-start.28 = (f32[2048]{0:T(1024)S(1)}, f32[2048]{0:T(1024)}, u32[]{:S(2)}) copy-start(f32[2048]{0:T(1024)} %copy-done.27) | copy-start | bytes 24580
  1029.0 384.9 %copy-start.30 = (f32[2048]{0:T(1024)S(1)}, f32[2048]{0:T(1024)}, u32[]{:S(2)}) copy-start(f32[2048]{0:T(1024)} %copy-done.29) | copy-start | bytes 24580
  1029.1 384.9 %copy-start.35 = (pred[2048]{0:T(1024)(128)(4,1)S(1)}, pred[2048]{0:T(1024)(128)(4,1)}, u32[]{:S(2)}) copy-start(pred[2048]{0:T(1024)(128)(4,1)} %copy-done.34) | copy-start | bytes 6148
  1029.1 384.9 %copy-start.37 = (pred[2048]{0:T(1024)(128)(4,1)S(1)}, pred[2048]{0:T(1024)(128)(4,1)}, u32[]{:S(2)}) copy-start(pred[2048]{0:T(1024)(128)(4,1)} %copy-done.36) | copy-start | bytes 6148
  1029.1 384.9 %copy-start.39 = (pred[2048]{0:T(1024)(128)(4,1)S(1)}, pred[2048]{0:T(1024)(128)(4,1)}, u32[]{:S(2)}) copy-start(pred[2048]{0:T(1024)(128)(4,1)} %copy-done.38) | copy-start | bytes 6148
  1029.1 384.9 %copy-start.41 = (pred[2048]{0:T(1024)(128)(4,1)S(1)}, pred[2048]{0:T(1024)(128)(4,1)}, u32[]{:S(2)}) copy-start(pred[2048]{0:T(1024)(128)(4,1)} %copy-done.40) | copy-start | bytes 6148
  1029.1 384.9 %copy-start.43 = (pred[2048]{0:T(1024)(128)(4,1)S(1)}, pred[2048]{0:T(1024)(128)(4,1)}, u32[]{:S(2)}) copy-start(pred[2048]{0:T(1024)(128)(4,1)} %copy-done.42) | copy-start | bytes 6148
  1029.1 384.9 %copy-start.45 = (pred[2048]{0:T(1024)(128)(4,1)S(1)}, pred[2048]{0:T(1024)(128)(4,1)}, u32[]{:S(2)}) copy-start(pred[2048]{0:T(1024)(128)(4,1)} %copy-done.44) | copy-start | bytes 6148
  1029.1 384.9 %copy-start.47 = (pred[2048]{0:T(1024)(128)(4,1)S(1)}, pred[2048]{0:T(1024)(128)(4,1)}, u32[]{:S(2)}) copy-start(pred[2048]{0:T(1024)(128)(4,1)} %copy-done.46) | copy-start | bytes 6148
  1029.1 384.9 %copy-start.49 = (pred[2048]{0:T(1024)(128)(4,1)S(1)}, pred[2048]{0:T(1024)(128)(4,1)}, u32[]{:S(2)}) copy-start(pred[2048]{0:T(1024)(128)(4,1)} %copy-done.48) | copy-start | bytes 6148
  1029.1 384.9 %copy-start.51 = (s32[32]{0:T(128)S(1)}, s32[32]{0:T(128)}, u32[]{:S(2)}) copy-start(s32[32]{0:T(128)} %copy-done.50) | copy-start | bytes 388
  1032.8 379.3 %collective-permute-start.5 = (f32[2048,128]{1,0:T(8,128)}, f32[2048,128]{1,0:T(8,128)}, u32[]{:S(2)}, u32[]{:S(2)}) collective-permute-start(f32[2048,128]{1,0:T(8,128)} %add.101), channel_id=1, source_target_pairs={{0,8},{1,9},{2,10},{3,11},{4,12},{5,13},{6,14},{7,15},{8,0},{9,1},... | collective-permute-start | bytes 3145736 | tf_op jit(solution)/shard_map/ppermute | solution.py:145
  1431.8 33.8 %copy-start.10 = (bf16[1024,2,2,8]{0,3,2,1:T(8,128)(2,1)S(1)}, bf16[1024,2,2,8]{0,3,2,1:T(8,128)(2,1)}, u32[]{:S(2)}) copy-start(bf16[1024,2,2,8]{0,3,2,1:T(8,128)(2,1)} %copy-done.9) | copy-start | bytes 196612
  1431.8 53.2 %collective-permute-start.10 = (f32[776,1024]{1,0:T(8,128)}, f32[776,1024]{1,0:T(8,128)}, u32[]{:S(2)}, u32[]{:S(2)}) collective-permute-start(f32[776,1024]{1,0:T(8,128)} %broadcast_select_fusion.2), channel_id=1, source_target_pairs={{0,1},{1,0},{2,3},{3,2},{4,5},{5,4},{6,7},{7,6},{8,9},{9,8},{10,11... | collective-permute-start | bytes 9535496 | tf_op jit(solution)/shard_map/ppermute | solution.py:202
  1432.7 5.3 collective-permute-start.6
  1438.0 10.4 collective-permute-start.7
  1448.4 10.2 collective-permute-start.8
  1458.6 5.4 collective-permute-start.9
  (38 other events, 237.1 us)
Sparse Core Ops, SparseCore 0:
  14.6 123.0 all-gather.6
  140.1 121.4 all-gather.4
  1025.9 151.9 reduce-scatter.7
  1181.2 151.8 reduce-scatter.5
  1336.6 284.5 reduce-scatter.3
